TPU v7x, 512 devices: a whole 4x4x16 slice. The times are simulated.
512 devices in a mesh: doc: 8 (over x, core), seq: 64 (over z, y).
Axes of the slice: x: 4, y: 4, z: 16, core: 2. Of those that a mesh axis runs over, the one named last changes fastest.
Arguments:
- queries: bfloat16 [65536, 1792], P(('doc', 'seq')), parts along dimension 0, may hold values from -5 to 5
- keys: bfloat16 [65536, 256], P(('doc', 'seq')), parts along dimension 0, may hold values from -5 to 5
- values: bfloat16 [65536, 256], P(('doc', 'seq')), parts along dimension 0, may hold values from -6 to 6
- doc_length: int32 [8], P('doc'), parts along dimension 0, may hold values from 4096 to 8192
- sink_pos: int32 [32], P('doc'), parts along dimension 0, may hold values from 0 to 127, as said below
Outputs:
- attended: bfloat16 [65536, 1792], P(('doc', 'seq')), parts along dimension 0
- row_lse: float32 [14, 65536], P(None, ('doc', 'seq')), parts along dimension 1
- sink_mass: float32 [14, 65536], P(None, ('doc', 'seq')), parts along dimension 1
- head_lse: float32 [112], P('doc'), parts along dimension 0
- head_sink: float32 [112], P('doc'), parts along dimension 0
There are 8 independent parts, one for each index of `doc`. A program takes and returns all parts, laid end to end along the dimension named above; each array names one. Nothing has to cross between parts.
Inputs may be any that keep to these rules, and one draw needn't show every extreme that they name: `sink_pos`: 4 distinct positions within the document's first 128 tokens; positions 0 and 127 are always among them. Positions from doc_length up to 8192 are padding.
All inputs are finite; a program needn't handle non-finite values.
Results may differ from a plain program's by a relative error of at most 0.009.
Values may be sent and summed in bfloat16 or wider, within the bound.
A program may use at most 64 MiB of HBM per device.

v0:
```python
import jax
import jax.numpy as jnp
from jax import lax
from jax.sharding import PartitionSpec as P

HEAD_DIMENSION = 128


def side_by_side(arrays, axis, dim, along):
    widths = [a.shape[along] for a in arrays]
    both = jnp.concatenate(arrays, axis=along)
    filled = lax.all_gather(both, axis, axis=dim, tiled=True)
    return tuple(jnp.split(filled, [sum(widths[:k]) for k in range(1, len(widths))], axis=along))


def picked(value, axis, root):
    return lax.dynamic_index_in_dim(lax.all_gather(value, axis), root, 0, keepdims=False)


def from_everyone(value, axis):
    count = lax.axis_size(axis)
    return lax.all_to_all(
        jnp.broadcast_to(value[None], (count, *value.shape)), axis, 0, 0, tiled=True
    )


def taken_together(value, axis):
    everything = from_everyone(value, axis)
    return jnp.sum(everything, axis=0)


def in_one(arrays, axis):
    ends = [0]
    for a in arrays:
        ends.append(ends[-1] + a.size)
    so_far = taken_together(jnp.concatenate([a.ravel() for a in arrays]), axis)
    return tuple((so_far[b:e].reshape(a.shape) for a, b, e in zip(arrays, ends, ends[1:])))


def body(queries, keys, values, doc_length, sink_pos):
    my_index = lax.axis_index("seq")
    row_count = queries.shape[0]
    head_count = queries.shape[1] // HEAD_DIMENSION
    key_heads = keys.shape[1] // HEAD_DIMENSION
    query_group_width = head_count // key_heads
    length = doc_length[0]
    offsets = jnp.arange(row_count, dtype=jnp.int32)
    row_pos = my_index * row_count + offsets
    grouped = queries.reshape(row_count, key_heads, query_group_width, HEAD_DIMENSION).transpose(
        1, 2, 0, 3
    )
    grouped = grouped.reshape(key_heads, query_group_width * row_count, HEAD_DIMENSION)
    flat_pos = jnp.tile(row_pos, query_group_width)
    needed = jnp.minimum(jnp.max(row_pos), length - 1)
    score_scale = HEAD_DIMENSION ** (-0.5)

    def attend(running, key_block, value_block, first_row):
        run_max, run_sum, weighted, sink_sum = running
        rows_per_block = key_block.shape[0]
        key_pos = first_row + jnp.arange(rows_per_block, dtype=jnp.int32)
        key_mat = key_block.reshape(rows_per_block, key_heads, HEAD_DIMENSION)
        value_mat = value_block.reshape(rows_per_block, key_heads, HEAD_DIMENSION)
        scores = (
            jnp.einsum("gqd,pgd->gqp", grouped, key_mat, preferred_element_type=jnp.float32)
            * score_scale
        )
        allowed = (key_pos[None, :] <= flat_pos[:, None]) & (key_pos[None, :] < length)
        block_max = jnp.max(jnp.where(allowed[None], scores, -1e30), axis=-1)
        new_max = jnp.maximum(run_max, block_max)
        rescale = jnp.exp(run_max - new_max)
        weights = jnp.where(allowed[None], jnp.exp(scores - new_max[..., None]), 0.0)
        run_sum = run_sum * rescale + jnp.sum(weights, axis=-1)
        weighted = weighted * rescale[..., None] + jnp.einsum(
            "gqp,pgd->gqd",
            weights.astype(jnp.bfloat16),
            value_mat,
            preferred_element_type=jnp.float32,
        )
        return (new_max, run_sum, weighted, sink_sum)

    def guarded(running, key_block, value_block, first_row):
        return lax.cond(
            first_row <= needed,
            lambda current: attend(current, key_block, value_block, first_row),
            lambda current: current,
            running,
        )

    stat_shape = (key_heads, query_group_width * row_count)
    initial = (
        jnp.full(stat_shape, -1e30, jnp.float32),
        jnp.zeros(stat_shape, jnp.float32),
        jnp.zeros(stat_shape + (HEAD_DIMENSION,), jnp.float32),
        jnp.zeros(stat_shape, jnp.float32),
    )
    running = initial
    key_piece, value_piece = side_by_side((keys, values), "seq", 0, 1)
    piece_rows = key_piece.shape[0]
    block_width = 512
    full_blocks = piece_rows // block_width
    key_stack = key_piece.reshape(full_blocks, block_width, key_piece.shape[1])
    value_stack = value_piece.reshape(full_blocks, block_width, value_piece.shape[1])

    def scan_step(current, packed):
        key_block, value_block, block_index = packed
        return (guarded(current, key_block, value_block, block_index * block_width), None)

    running, _ = lax.scan(
        scan_step, running, (key_stack, value_stack, jnp.arange(full_blocks, dtype=jnp.int32))
    )
    run_max, run_sum, weighted, sink_sum = running
    row_lse = run_max + jnp.log(run_sum)
    attended = (weighted / run_sum[..., None]).reshape(
        key_heads, query_group_width, row_count, HEAD_DIMENSION
    )
    attended = attended.transpose(2, 0, 1, 3).reshape(row_count, head_count * HEAD_DIMENSION)
    live_rows = row_pos < length
    attended = jnp.where(live_rows[:, None], attended, 0.0).astype(jnp.bfloat16)
    local_sinks = keys[sink_pos]
    sink_keys = picked(local_sinks, "seq", 0).reshape(sink_pos.shape[0], key_heads, HEAD_DIMENSION)
    sink_scores = (
        jnp.einsum("gqd,ngd->gqn", grouped, sink_keys, preferred_element_type=jnp.float32)
        * score_scale
    )
    reachable = sink_pos[None, :] <= flat_pos[:, None]
    sink_mass = jnp.sum(
        jnp.where(reachable[None], jnp.exp(sink_scores - row_lse[..., None]), 0.0), axis=-1
    )
    row_lse = jnp.where(live_rows[None, :], row_lse.reshape(head_count, row_count), 0.0)
    sink_mass = jnp.where(live_rows[None, :], sink_mass.reshape(head_count, row_count), 0.0)
    totals = in_one((jnp.sum(row_lse, axis=1), jnp.sum(sink_mass, axis=1)), "seq")
    doc_count = length.astype(jnp.float32)
    head_lse = totals[0] / doc_count
    head_sink = totals[1] / doc_count
    return (attended, row_lse, sink_mass, head_lse, head_sink)


def solution(mesh):
    placed = (
        P(("doc", "seq"), None),
        P(("doc", "seq"), None),
        P(("doc", "seq"), None),
        P("doc"),
        P("doc"),
    )
    return jax.shard_map(
        body,
        mesh=mesh,
        in_specs=placed,
        out_specs=(
            P(("doc", "seq"), None),
            P(None, ("doc", "seq")),
            P(None, ("doc", "seq")),
            P("doc"),
            P("doc"),
        ),
        check_vma=False,
    )
```

profile of v0, /device:TPU:8, one launch (start us, length us, event | category | flops | bytes accessed | tf_op | source)
XLA Modules:
  0.0 329.7 jit_solution(10629638236363354667)
XLA Ops:
  7.2 0.0 all-gather.4.cloned.1.call-start
  7.2 1.5 pad_maximum_fusion
  8.7 0.0 all-gather.4.cloned.1.call-update
  9.4 1.3 copy.58
  10.7 0.3 copy.59
  11.0 0.7 compare_select_fusion
  11.6 1.4 gather_fusion
  13.1 0.6 iota_add_fusion.1
  14.3 106.1 %all-gather.1 = bf16[64,4,256]{2,1,0:T(4,128)(2,1)S(1)} all-gather(bf16[1,4,256]{2,1,0:T(4,128)(2,1)S(1)} %bitcast.63), channel_id=2, replica_groups=mesh['doc'=8,'seq'=64] {'seq'}, dimensions={0}, use_global_device_ids=true | all-gather | bytes 133120 | tf_op jit(solution)/shard_map/all_gather | solution.py:17
  120.5 0.7 broadcast_compare_fusion.1
  121.2 49.5 %all-gather.4.cloned.1.call-done = bf16[8192,512]{1,0:T(8,128)(2,1)} async-done(((bf16[128,512]{1,0:T(8,128)(2,1)}), bf16[8192,512]{1,0:T(8,128)(2,1)}) %all-gather.4.cloned.1.call-update) | async-done | bytes 8388624 | tf_op jit(solution)/shard_map/all_gather | solution.py:12
  170.7 5.7 %fusion.27 = (bf16[8192,256]{1,0:T(8,128)(2,1)}, bf16[8192,256]{1,0:T(8,128)(2,1)}) fusion(bf16[8192,512]{1,0:T(8,128)(2,1)} %all-gather.4.cloned.1.call-done), kind=kLoop, calls=%fused_computation.51 | loop fusion | bytes 16777216 | tf_op jit(solution)/shard_map/split | solution.py:13
  176.4 6.4 %copy.60 = bf16[16,512,256]{1,2,0:T(8,128)(2,1)} copy(bf16[16,512,256]{2,1,0:T(8,128)(2,1)} %bitcast.59) | data formatting | bytes 8388608
  182.8 6.4 %copy.61 = bf16[16,512,256]{1,2,0:T(8,128)(2,1)} copy(bf16[16,512,256]{2,1,0:T(8,128)(2,1)} %bitcast.58) | data formatting | bytes 8388608
  189.3 0.1 broadcast_in_dim.99
  189.4 26.1 %while.15 = (s32[]{:T(128)}, f32[2,896]{1,0:T(2,128)S(1)}, f32[2,896]{1,0:T(2,128)S(1)}, f32[2,896,128]{2,1,0:T(8,128)S(1)}, s32[16]{0:T(128)S(1)}, /*index=5*/s...) while((s32[]{:T(128)}, f32[2,896]{1,0:T(2,128)S(1)}, ...), condition=%wide.region_6.7_spmd.clone, body=%wide.region_1.6_spmd.clone.sunk | while | flops 481235968 | bytes 16839484 | solution.py:108
  189.4 0.6 dynamic_slice.30
  190.6 5.6 %conditional.3 = ((f32[2,896]{1,0:T(2,128)S(1)}, f32[2,896]{1,0:T(2,128)S(1)}, f32[2,896,128]{2,1,0:T(8,128)S(1)})) conditional(s32[]{:T(128)} %convert_element_type.23, (f32[2,896]{1,0:T(2,128)S(1)}, f32[2,896]{1,0:T(2,128)S(1)}, f32[2,896,128]{2,1,0:T(8,128)S(1)}) %tuple.61, (s32[]{:T(128)}, s32[128]{0:T(128)S(1)}, s32[]{:T(128)}, ...), branch_computations={%region_2.2_spmd, %region_3.5_spmd} | conditional | flops 481235968 | bytes 16839216 | solution.py:82
  190.6 0.7 broadcast_compare_fusion
  191.3 0.4 compare_and_fusion
  191.7 1.1 constant_dynamic-slice_fusion
  192.8 1.0 fusion.2
  193.8 0.9 fusion.6
  194.7 1.6 fusion.13
  196.3 0.6 dynamic_slice.30
  197.5 0.6 dynamic_slice.30
  198.8 0.6 dynamic_slice.30
  200.1 0.6 dynamic_slice.30
  201.4 0.6 dynamic_slice.30
  202.7 0.6 dynamic_slice.30
  204.0 0.6 dynamic_slice.30
  205.2 0.6 dynamic_slice.30
  206.5 0.6 dynamic_slice.30
  207.8 0.6 dynamic_slice.30
  209.1 0.6 dynamic_slice.30
  210.4 0.6 dynamic_slice.30
  211.7 0.6 dynamic_slice.30
  212.9 0.6 dynamic_slice.30
  214.2 0.6 dynamic_slice.30
  215.5 0.3 fusion.22
  215.8 0.7 fusion.26
  216.5 0.1 pad_maximum_fusion.1
  216.6 0.6 broadcast_in_dim.106
  217.2 91.2 %all-to-all-start = ((f32[64,1,28]{2,1,0:T(1,128)}), f32[64,1,28]{2,1,0:T(1,128)S(1)}, u32[]{:S(2)}, u32[]{:S(2)}) async-start(f32[64,1,28]{2,1,0:T(1,128)} %broadcast_in_dim.106), calls=%async_computation | async-start | bytes 65536 | tf_op jit(solution)/shard_map/all_to_all | solution.py:22
  308.5 0.3 broadcast_divide_fusion
  308.8 0.3 copy.62
  309.1 0.1 fusion.23
  309.2 1.0 copy.64
  310.2 12.0 %all-to-all-done = f32[64,1,28]{2,1,0:T(1,128)S(1)} async-done(((f32[64,1,28]{2,1,0:T(1,128)}), f32[64,1,28]{2,1,0:T(1,128)S(1)}, u32[]{:S(2)}, u32[]{:S(2)}) %all-to-all-start) | async-done | bytes 7200 | tf_op jit(solution)/shard_map/all_to_all | solution.py:22
  322.2 0.1 reduce_sum.50
  322.3 0.6 slice_divide_fusion
  (29 shorter events, 0.3 us)
Async XLA Ops:
  7.2 163.6 %all-gather.4.cloned.1.call-start = ((), (), s32[]{:S(2)}) async-start(), calls=%async_computation.1 | async-start | bytes 8519680 | tf_op jit(solution)/shard_map/all_gather | solution.py:12
  217.2 104.9 %all-to-all-start = ((f32[64,1,28]{2,1,0:T(1,128)}), f32[64,1,28]{2,1,0:T(1,128)S(1)}, u32[]{:S(2)}, u32[]{:S(2)}) async-start(f32[64,1,28]{2,1,0:T(1,128)} %broadcast_in_dim.106), calls=%async_computation | async-start | bytes 65536 | tf_op jit(solution)/shard_map/all_to_all | solution.py:22
Sparse Core Ops, SparseCore 0:
  11.5 159.1 all-gather.3
where the time goes:
time: 331 us; the launch traced here: 330 us
  blocking collectives  106 us (32%)
  starting transfers between devices  91.3 us (28%)
  waiting for transfers between devices  61.5 us (19%)
  local copies, waits for them, and re-layouts  33.9 us (10%)
  between operations  15.4 us (5%)
  loops' own time  11.2 us (3%)
  other arithmetic  7.4 us (2%)
    all_gather x1, blocking collectives, picked(): lax.all_gather(value, axis)  106 us
    all_to_all x1, starting transfers between devices, from_everyone(): lax.all_to_all(jnp.broadcast_to(value[None], (count, *value.shape)), axis...  91.2 us
    all_gather x1, waiting for transfers between devices, side_by_side(): filled = lax.all_gather(both, axis, axis=dim, tiled=True)  49.5 us
    unnamed x4, local copies, waits for them, and re-layouts  15.1 us
    all_to_all x1, waiting for transfers between devices, from_everyone(): lax.all_to_all(jnp.broadcast_to(value[None], (count, *value.shape)), axis...  12 us
    another operation x1, loops' own time, body(): lax.scan(scan_step, running, (key_stack, value_stack, jnp.arange(full_blo...  10.9 us
    dynamic_slice x17, local copies, waits for them, and re-layouts, body(): lax.scan(scan_step, running, (key_stack, value_stack, jnp.arange(full_blo...  10.5 us
  transfers between devices with their start and end apart: 2, of which 2 were waited for; matrix products, arithmetic and copies ran while one was open for 2% of the time, Pallas kernels for 0%

commit v1 on v0

v1 whole, which is shorter than its diff:
```python
import functools

import jax
import jax.numpy as jnp
from jax import lax
from jax.experimental import pallas as pl
from jax.experimental.pallas import tpu as pltpu
from jax.sharding import PartitionSpec as P

MESH = pl.DeviceIdType.MESH
D = 128
R = 128
NY = 4
HG = 7
CW = HG * D
SCALE = D**-0.5
LC = SCALE * 1.4426950408889634
LOW = -(2.0**60)


def gray(i):
    return i + (i // 2) * (1 - 2 * (i % 2))


def kernel(
    NZ,
    len_ref,
    sink_ref,
    q_hbm,
    k_hbm,
    v_hbm,
    out_ref,
    lse_ref,
    mass_ref,
    hl_ref,
    hs_ref,
    qbuf,
    qx,
    kbuf,
    vbuf,
    kx,
    vx,
    ebuf,
    m_ref,
    acc_ref,
    osend,
    xsend,
    orecv,
    xrecv,
    xs_ref,
    pk_ref,
    ysum,
    zsum,
    loc_sem,
    qs_sem,
    qr_sem,
    xk_sem,
    kr_sem,
    vr_sem,
    kus,
    vus,
    kds,
    vds,
    os_sem,
    or_sem,
    ss_sem,
    sr_sem,
    ys_sem,
    yr_sem,
    zs_sem,
    zr_sem,
):
    NU = NZ // 2
    ND = NU - 1
    KD = NU - 2
    NST = NU // 2
    s = lax.axis_index("seq")
    z = s // NY
    y = s % NY
    g = y % 2
    b = y // 2

    def dev(zz, yy):
        return {"seq": zz * NY + yy}

    def lanes(ref, start, size):
        return ref.at[:, pl.ds(pl.multiple_of(start, 128), size)]

    c0 = pltpu.make_async_copy(lanes(k_hbm, g * D, D), kbuf.at[pl.ds(pl.multiple_of(g * R, R), R), :], loc_sem.at[0])
    c1 = pltpu.make_async_copy(lanes(v_hbm, g * D, D), vbuf.at[pl.ds(pl.multiple_of(g * R, R), R), :], loc_sem.at[1])
    c2 = pltpu.make_async_copy(lanes(k_hbm, (1 - g) * D, D), kx, loc_sem.at[2])
    c3 = pltpu.make_async_copy(lanes(v_hbm, (1 - g) * D, D), vx, loc_sem.at[3])
    c4 = pltpu.make_async_copy(lanes(q_hbm, (1 - g) * CW, CW), qx, loc_sem.at[4])
    c5 = pltpu.make_async_copy(lanes(q_hbm, g * CW, CW), qbuf.at[y], loc_sem.at[5])
    for c in (c0, c1, c2, c3, c4, c5):
        c.start()

    barrier = pltpu.get_barrier_semaphore()

    def greet_z(i, _):
        pl.semaphore_signal(barrier, inc=1, device_id=dev((z + i) % NZ, y), device_id_type=MESH)
        return 0

    def greet_y(i, _):
        pl.semaphore_signal(barrier, inc=1, device_id=dev(z, (y + i) % NY), device_id_type=MESH)
        return 0

    lax.fori_loop(1, NY, greet_y, 0)
    lax.fori_loop(1, NZ, greet_z, 0)

    lane = lax.broadcasted_iota(jnp.int32, (2 * R, D), 1)
    row = lax.broadcasted_iota(jnp.int32, (2 * R, D), 0)
    plain = jnp.where(lane < 64, 1.0, 0.0).astype(jnp.bfloat16)

    def fill(i, _):
        ebuf[pl.ds(pl.multiple_of(i * 2 * R, 2 * R), 2 * R), :] = plain
        return 0

    lax.fori_loop(0, NZ, fill, 0)
    kpos = row + b * 2 * R
    hit = kpos == sink_ref[0]
    for n in range(1, 4):
        hit = hit | (kpos == sink_ref[n])
    first = jnp.where(z < NU + 1, z, NZ + 1 - z)
    ebuf[pl.ds(pl.multiple_of(first * 2 * R, 2 * R), 2 * R), :] = jnp.where(
        (lane < 64) | hit, 1.0, 0.0
    ).astype(jnp.bfloat16)

    for c in (c0, c1, c2, c3, c4, c5):
        c.wait()
    pl.semaphore_wait(barrier, NY - 1 + NZ - 1)

    def cell(ref, slot, c):
        return ref.at[pl.ds(pl.multiple_of(slot * (2 * R) + c * R, R), R), :]

    def up_slot(zz, j):
        return j + jnp.maximum(0, j - (NZ - zz))

    def down_slot(zz, j):
        return jnp.where(zz + j >= NZ, 2 * j + 1 - (NZ - zz), NZ + j)

    def pair(slot, tslot, c, ss, vs, j, zt, yt):
        return (
            pltpu.make_async_remote_copy(
                src_ref=cell(kbuf, slot, c),
                dst_ref=cell(kbuf, tslot, c),
                send_sem=ss.at[j, c],
                recv_sem=kr_sem.at[tslot, c],
                device_id=dev(zt, yt),
                device_id_type=MESH,
            ),
            pltpu.make_async_remote_copy(
                src_ref=cell(vbuf, slot, c),
                dst_ref=cell(vbuf, tslot, c),
                send_sem=vs.at[j, c],
                recv_sem=vr_sem.at[tslot, c],
                device_id=dev(zt, yt),
                device_id_type=MESH,
            ),
        )

    def up(slot, c, j):
        return pair(slot, up_slot(z + 1, j + 1), c, kus, vus, j, (z + 1) % NZ, y)

    def down(slot, c, j):
        zt = (z + NZ - 1) % NZ
        return pair(slot, down_slot(zt, j + 1), c, kds, vds, j, zt, y)

    def start_up(slot, c, j):
        @pl.when((j < NU) & (z < NZ - 1) & (z >= j))
        def _():
            for d in up(slot, c, j):
                d.start()

    def start_down(slot, c, j):
        @pl.when((j < ND) & ((z + j) % NZ <= KD))
        def _():
            for d in down(slot, c, j):
                d.start()

    start_up(0, g, 0)
    start_down(0, g, 0)

    yp = y + 1 - 2 * g
    to_pair = (
        pltpu.make_async_remote_copy(
            src_ref=kx, dst_ref=cell(kbuf, 0, g), send_sem=xk_sem.at[0], recv_sem=kr_sem.at[0, g],
            device_id=dev(z, yp), device_id_type=MESH,
        ),
        pltpu.make_async_remote_copy(
            src_ref=vx, dst_ref=cell(vbuf, 0, g), send_sem=xk_sem.at[1], recv_sem=vr_sem.at[0, g],
            device_id=dev(z, yp), device_id_type=MESH,
        ),
    )
    for d in to_pair:
        d.start()

    def q_copy(i):
        src = qbuf.at[y] if i == 2 else qx
        return pltpu.make_async_remote_copy(
            src_ref=src, dst_ref=qbuf.at[y], send_sem=qs_sem.at[i], recv_sem=qr_sem.at[y],
            device_id=dev(z, (y + i) % NY), device_id_type=MESH,
        )

    for i in (1, 3, 2):
        q_copy(i).start()

    def wait_cell(slot, c):
        for ref, sem in ((kbuf, kr_sem), (vbuf, vr_sem)):
            pltpu.make_async_remote_copy(
                src_ref=cell(ref, slot, c), dst_ref=cell(ref, slot, c), send_sem=xk_sem.at[0],
                recv_sem=sem.at[slot, c], device_id=dev(z, yp), device_id_type=MESH,
            ).wait_recv()

    def wait_q(t):
        pltpu.make_async_remote_copy(
            src_ref=qx, dst_ref=qbuf.at[t], send_sem=qs_sem.at[0], recv_sem=qr_sem.at[t],
            device_id=dev(z, yp), device_id_type=MESH,
        ).wait_recv()

    wait_cell(0, 1 - g)
    start_up(0, 1 - g, 0)
    start_down(0, 1 - g, 0)

    def poll(e):
        j = e // 2 + 1
        c = (g + e) % 2

        @pl.when(z >= j)
        def _():
            slot = up_slot(z, j)
            wait_cell(slot, c)
            start_up(slot, c, j)

        @pl.when((j <= ND) & ((z + j) % NZ <= KD))
        def _():
            slot = down_slot(z, j)
            wait_cell(slot, c)
            start_down(slot, c, j)

    def scores(t, h, k):
        return lax.dot_general(
            qbuf[t, :, h * D : (h + 1) * D], k, (((1,), (1,)), ((), ())), preferred_element_type=jnp.float32
        )

    def weigh(sc, mn):
        mc = mn * LC
        cols = [jnp.exp2(sc[:, n * D : (n + 1) * D] * LC - mc) for n in range(sc.shape[1] // D)]
        return jnp.concatenate(cols, axis=1).astype(jnp.bfloat16)

    def mix(p, ve):
        return lax.dot_general(p, ve, (((1,), (0,)), ((), ())), preferred_element_type=jnp.float32)

    qi = lax.broadcasted_iota(jnp.int32, (R, 2 * R), 0)
    ki = lax.broadcasted_iota(jnp.int32, (R, 2 * R), 1)

    def attend_own(t):
        k = kbuf[0 : 2 * R, :]
        ve = jnp.concatenate([vbuf[0 : 2 * R, :], ebuf[0 : 2 * R, :]], axis=1)
        ok = ki + b * 2 * R <= qi + t * R
        sc = [jnp.where(ok, scores(t, h, k), LOW) for h in range(HG)]
        for h in range(HG):
            mn = jnp.broadcast_to(jnp.max(sc[h], axis=1, keepdims=True), (R, D))
            m_ref[t, h] = mn
            acc_ref[t, h] = mix(weigh(sc[h], mn), ve)

    def attend(t, base, n):
        rows = pl.ds(pl.multiple_of(base, 2 * R), n * 2 * R)
        k = kbuf[rows, :]
        ve = jnp.concatenate([vbuf[rows, :], ebuf[rows, :]], axis=1)
        sc = [scores(t, h, k) for h in range(HG)]
        for h in range(HG):
            mo = m_ref[t, h]
            mn = jnp.maximum(mo, jnp.max(sc[h], axis=1, keepdims=True))
            al = jnp.exp2((mo - mn) * LC)
            pv = mix(weigh(sc[h], mn), ve)
            acc_ref[t, h] = acc_ref[t, h] * jnp.concatenate([al, al], axis=1) + pv
            m_ref[t, h] = mn

    def own_step(i, _):
        t = (y + gray(i)) % NY

        @pl.when(i > 0)
        def _():
            wait_q(t)

        attend_own(t)
        poll(i)
        return 0

    lax.fori_loop(0, NY, own_step, 0)

    def have(st):
        return jnp.minimum(2 * st, z) + jnp.maximum(0, jnp.minimum(2 * st, ND) - (NZ - z) + 1)

    lane1 = lax.broadcasted_iota(jnp.int32, (R, D), 1)

    def finish(t, gi):
        x = jnp.zeros((R, D), jnp.float32)
        for h in range(HG):
            a = acc_ref[t, h]
            total = jnp.broadcast_to(a[:, D : D + 1], (R, D))
            mass = jnp.broadcast_to(a[:, D + 64 : D + 65], (R, D))
            inv = 1.0 / total
            osend[gi, :, h * D : (h + 1) * D] = (a[:, :D] * inv).astype(jnp.bfloat16)
            x = jnp.where(lane1 == h, m_ref[t, h] * SCALE + jnp.log(total), x)
            x = jnp.where(lane1 == 8 + h, mass * inv, x)
        xs_ref[...] = x.T
        xsend[gi] = xs_ref[0:16, :]

    def back(gi):
        t = (y + gi) % NY
        return (
            pltpu.make_async_remote_copy(
                src_ref=xsend.at[gi], dst_ref=xrecv.at[y], send_sem=ss_sem.at[gi], recv_sem=sr_sem.at[y],
                device_id=dev(z, t), device_id_type=MESH,
            ),
            pltpu.make_async_remote_copy(
                src_ref=osend.at[gi], dst_ref=orecv.at[y], send_sem=os_sem.at[gi], recv_sem=or_sem.at[y],
                device_id=dev(z, t), device_id_type=MESH,
            ),
        )

    def stage_step(it, _):
        st = it // NY + 1
        i = it % NY
        last = st == NST
        before = have(st - 1)
        count = have(st) - before
        gi = gray(jnp.where(last, NY - 1 - i, i))
        t = (y + gi) % NY
        for n in range(1, 5):

            @pl.when(count == n)
            def _():
                attend(t, (before + 1) * 2 * R, n)

        @pl.when(st < NST)
        def _():
            poll(NY * st + i)

        @pl.when(last)
        def _():
            finish(t, gi)

            @pl.when(gi > 0)
            def _():
                for d in back(gi):
                    d.start()

        return 0

    lax.fori_loop(0, NST * NY, stage_step, 0)

    xrecv[y] = xsend[0]
    for i in range(1, NY):
        yy = (y + i) % NY
        pltpu.make_async_remote_copy(
            src_ref=xsend.at[0], dst_ref=xrecv.at[yy], send_sem=ss_sem.at[0], recv_sem=sr_sem.at[yy],
            device_id=dev(z, yp), device_id_type=MESH,
        ).wait_recv()
    pos = s * R + lax.broadcasted_iota(jnp.int32, (8, D), 1)
    live = pos < len_ref[0]
    pk_ref[...] = jnp.zeros_like(pk_ref)
    for gg in range(2):
        xa, xb = xrecv[gg], xrecv[2 + gg]
        la, lb = xa[0:8], xb[0:8]
        top = jnp.maximum(la, lb)
        ea, eb = jnp.exp(la - top), jnp.exp(lb - top)
        tot = ea + eb
        wa, wb = ea / tot, eb / tot
        lse = jnp.where(live, top + jnp.log(tot), 0.0)
        mass = jnp.where(live, wa * xa[8:16] + wb * xb[8:16], 0.0)
        lse_ref[gg * HG : (gg + 1) * HG, :] = lse[0:HG]
        mass_ref[gg * HG : (gg + 1) * HG, :] = mass[0:HG]
        pk_ref[32 + 16 * gg : 40 + 16 * gg, :] = jnp.where(live, wa, 0.0)
        pk_ref[40 + 16 * gg : 48 + 16 * gg, :] = jnp.where(live, wb, 0.0)
    pk_ref[0 : 2 * HG, :] = lse_ref[...]
    pk_ref[16 : 16 + 2 * HG, :] = mass_ref[...]
    xs_ref[...] = pk_ref[...].T
    ysum[y] = jnp.broadcast_to(jnp.sum(xs_ref[...], axis=0, keepdims=True), (8, D))

    def sum_y(i):
        return pltpu.make_async_remote_copy(
            src_ref=ysum.at[y], dst_ref=ysum.at[y], send_sem=ys_sem.at[i], recv_sem=yr_sem.at[y],
            device_id=dev(z, (y + i) % NY), device_id_type=MESH,
        )

    for i in range(1, NY):
        sum_y(i).start()
    for i in range(1, NY):
        yy = (y + i) % NY
        pltpu.make_async_remote_copy(
            src_ref=ysum.at[y], dst_ref=ysum.at[yy], send_sem=ys_sem.at[0], recv_sem=yr_sem.at[yy],
            device_id=dev(z, yp), device_id_type=MESH,
        ).wait_recv()
    zsum[z] = ysum[0] + ysum[1] + ysum[2] + ysum[3]

    def sum_z(i):
        return pltpu.make_async_remote_copy(
            src_ref=zsum.at[z], dst_ref=zsum.at[z], send_sem=zs_sem.at[i], recv_sem=zr_sem.at[z],
            device_id=dev((z + i) % NZ, y), device_id_type=MESH,
        )

    def sum_z_start(i, _):
        sum_z(i).start()
        return 0

    lax.fori_loop(1, NZ, sum_z_start, 0)

    orecv[y] = osend[0]
    for i in range(1, NY):
        yy = (y + i) % NY
        pltpu.make_async_remote_copy(
            src_ref=osend.at[0], dst_ref=orecv.at[yy], send_sem=os_sem.at[0], recv_sem=or_sem.at[yy],
            device_id=dev(z, yp), device_id_type=MESH,
        ).wait_recv()
    for gg in range(2):
        for h in range(HG):
            at = 32 + 16 * gg + h
            cols = slice(h * D, (h + 1) * D)
            o = xs_ref[:, at : at + 1] * orecv[gg, :, cols].astype(jnp.float32)
            o = o + xs_ref[:, at + 8 : at + 9] * orecv[2 + gg, :, cols].astype(jnp.float32)
            out_ref[:, gg * CW + h * D : gg * CW + (h + 1) * D] = o.astype(jnp.bfloat16)

    def sum_z_wait(i, _):
        zz = (z + i) % NZ
        pltpu.make_async_remote_copy(
            src_ref=zsum.at[z], dst_ref=zsum.at[zz], send_sem=zs_sem.at[0], recv_sem=zr_sem.at[zz],
            device_id=dev(z, yp), device_id_type=MESH,
        ).wait_recv()
        return 0

    lax.fori_loop(1, NZ, sum_z_wait, 0)
    total = zsum[0]
    for i in range(1, NZ):
        total = total + zsum[i]
    mean = total[0:1, :] / len_ref[0].astype(jnp.float32)
    hl_ref[...] = mean[:, 0 : 2 * HG]
    hs_ref[...] = mean[:, 16 : 16 + 2 * HG]

    for c in range(2):
        for j in range(NU):

            @pl.when((z < NZ - 1) & (z >= j))
            def _():
                for d in up(0, c, j):
                    d.wait_send()

        for j in range(ND):

            @pl.when((z + j) % NZ <= KD)
            def _():
                for d in down(0, c, j):
                    d.wait_send()

    for d in to_pair:
        d.wait_send()
    for i in (1, 3, 2):
        q_copy(i).wait_send()
        sum_y(i).wait_send()
        for d in back(i):
            d.wait_send()

    def sum_z_sent(i, _):
        sum_z(i).wait_send()
        return 0

    lax.fori_loop(1, NZ, sum_z_sent, 0)


def body(queries, keys, values, doc_length, sink_pos):
    NZ = lax.axis_size("seq") // NY
    NU = NZ // 2
    cells = NZ + NU
    f32, bf16 = jnp.float32, jnp.bfloat16
    vm, dma = pltpu.VMEM, pltpu.SemaphoreType.DMA
    out, lse, mass, hl, hs = pl.pallas_call(
        functools.partial(kernel, NZ),
        out_shape=(
            jax.ShapeDtypeStruct((R, 2 * CW), bf16),
            jax.ShapeDtypeStruct((2 * HG, R), f32),
            jax.ShapeDtypeStruct((2 * HG, R), f32),
            jax.ShapeDtypeStruct((1, 2 * HG), f32),
            jax.ShapeDtypeStruct((1, 2 * HG), f32),
        ),
        in_specs=[
            pl.BlockSpec(memory_space=pltpu.SMEM),
            pl.BlockSpec(memory_space=pltpu.SMEM),
            pl.BlockSpec(memory_space=pl.ANY),
            pl.BlockSpec(memory_space=pl.ANY),
            pl.BlockSpec(memory_space=pl.ANY),
        ],
        out_specs=(pl.BlockSpec(memory_space=vm),) * 5,
        scratch_shapes=[
            vm((NY, R, CW), bf16),
            vm((R, CW), bf16),
            vm((cells * 2 * R, D), bf16),
            vm((cells * 2 * R, D), bf16),
            vm((R, D), bf16),
            vm((R, D), bf16),
            vm((NZ * 2 * R, D), bf16),
            vm((NY, HG, R, D), f32),
            vm((NY, HG, R, 2 * D), f32),
            vm((NY, R, CW), bf16),
            vm((NY, 16, R), f32),
            vm((NY, R, CW), bf16),
            vm((NY, 16, R), f32),
            vm((R, D), f32),
            vm((D, R), f32),
            vm((NY, 8, D), f32),
            vm((NZ, 8, D), f32),
            dma((6,)),
            dma((NY,)),
            dma((NY,)),
            dma((2,)),
            dma((cells, 2)),
            dma((cells, 2)),
            dma((NU, 2)),
            dma((NU, 2)),
            dma((NU, 2)),
            dma((NU, 2)),
            dma((NY,)),
            dma((NY,)),
            dma((NY,)),
            dma((NY,)),
            dma((NY,)),
            dma((NY,)),
            dma((NZ,)),
            dma((NZ,)),
        ],
        compiler_params=pltpu.CompilerParams(
            collective_id=0, has_side_effects=True, vmem_limit_bytes=56 * 2**20
        ),
    )(doc_length, sink_pos, queries, keys, values)
    return out, lse, mass, hl.reshape(2 * HG), hs.reshape(2 * HG)


def solution(mesh):
    rows = P(("doc", "seq"), None)
    return jax.shard_map(
        body,
        mesh=mesh,
        in_specs=(rows, rows, rows, P("doc"), P("doc")),
        out_specs=(rows, P(None, ("doc", "seq")), P(None, ("doc", "seq")), P("doc"), P("doc")),
        check_vma=False,
    )
```

time: 331 us -> 79.5 us (0.24)
  the two profiles are of different devices: /device:TPU:8 before, /device:TPU:6 now
where the time goes in v1:
time: 79.5 us; the launch traced here: 79.2 us
  Pallas kernels  73.7 us (93%)
  local copies, waits for them, and re-layouts  4.26 us (5%)
  between operations  1.3 us (2%)
    pallas_call x1, Pallas kernels, body(): pl.pallas_call(functools.partial(kernel, NZ), out_shape=(jax.ShapeDtypeSt...  73.7 us
    unnamed x13, local copies, waits for them, and re-layouts  4.26 us

profile of v1, /device:TPU:6, one launch (start us, length us, event | category | flops | bytes accessed | tf_op | source)
XLA Modules:
  0.0 79.2 jit_solution(1453256860891029472)
XLA Ops:
  1.3 73.7 %shard_map.92 = (bf16[128,1792]{1,0:T(8,128)(2,1)}, f32[14,128]{1,0:T(8,128)}, f32[14,128]{1,0:T(8,128)}, f32[1,14]{1,0:T(1,128)}, f32[1,14]{1,0:T(1,128)}) custom-call(s32[1]{0:T(128)S(6)} %copy.15.len_ref, s32[4]{0:T(128)} %sink_ref.1, bf16[128,1792]{1,0:T(8,128)(2,1)} %q_hbm.1, bf16[128,256]{1,0:T(8,128)(2,1)} %k_hbm.1, bf16[128,256]{1,0:T(8,128)(2,1)} %v_hbm.1), custom_call_target="tpu_custom_call" | custom-call | tf_op jit(solution)/shard_map/pallas_call | solution.py:478
  75.0 0.0 copy-start.1
  75.0 1.8 %copy.16 = bf16[128,1792]{1,0:T(8,128)(2,1)} copy(bf16[128,1792]{1,0:T(8,128)(2,1)} %get-tuple-element.20) | data formatting | bytes 917504
  76.8 0.0 copy-done.1
  76.8 0.0 copy-start
  76.8 0.6 copy.17
  77.4 0.1 copy-done
  77.5 0.0 copy-start.3
  77.5 0.6 copy.18
  78.1 0.0 copy-done.3
  78.1 0.0 copy-start.2
  78.1 0.5 copy.19
  78.7 0.1 copy-done.2
  78.7 0.5 copy.20
Async XLA Ops:
  75.0 1.8 %copy-start.1 = (f32[14,128]{1,0:T(8,128)S(1)}, f32[14,128]{1,0:T(8,128)}, u32[]{:S(2)}) copy-start(f32[14,128]{1,0:T(8,128)} %get-tuple-element.21) | copy-start | bytes 21508
  76.8 0.7 copy-start
  77.5 0.6 copy-start.3
  78.1 0.6 copy-start.2

commit v2 on v1

v2 whole, which is shorter than its diff:
```python
import functools

import jax
import jax.numpy as jnp
from jax import lax
from jax.experimental import pallas as pl
from jax.experimental.pallas import tpu as pltpu
from jax.sharding import PartitionSpec as P

MESH = pl.DeviceIdType.MESH
D = 128
R = 128
NY = 4
HG = 7
CW = HG * D
SCALE = D**-0.5
LC = SCALE * 1.4426950408889634
LOW = -(2.0**60)


def gray(i):
    return i + (i // 2) * (1 - 2 * (i % 2))


def kernel(
    NZ,
    len_hbm,
    sink_hbm,
    q_hbm,
    k_hbm,
    v_hbm,
    out_hbm,
    lse_hbm,
    mass_hbm,
    hl_hbm,
    hs_hbm,
    len_ref,
    sink_ref,
    lse_ref,
    mass_ref,
    hl_ref,
    hs_ref,
    qbuf,
    qx,
    kbuf,
    vbuf,
    kx,
    vx,
    ebuf,
    m_ref,
    acc_ref,
    osend,
    orecv,
    obuf,
    xrecv,
    xs_ref,
    pk_ref,
    zsum,
    loc_sem,
    qs_sem,
    qr_sem,
    xk_sem,
    kr_sem,
    vr_sem,
    kus,
    vus,
    kds,
    vds,
    os_sem,
    or_sem,
    ss_sem,
    sr_sem,
    zs_sem,
    zr_sem,
    hello,
):
    NU = NZ // 2
    ND = NU - 1
    KD = NU - 2
    NST = NU // 2
    s = lax.axis_index("seq")
    z = s // NY
    y = s % NY
    g = y % 2
    b = y // 2

    def dev(zz, yy):
        return {"seq": zz * NY + yy}

    def lanes(ref, start, size):
        return ref.at[:, pl.ds(pl.multiple_of(start, 128), size)]

    barrier = pltpu.get_barrier_semaphore()

    beside = ((z + 1) % NZ, (z + NZ - 1) % NZ)
    for zz in beside:
        pl.semaphore_signal(barrier, inc=1, device_id=dev(zz, y), device_id_type=MESH)
    for i in range(1, NY):
        pl.semaphore_signal(barrier, inc=1, device_id=dev(z, (y + i) % NY), device_id_type=MESH)

    c0 = pltpu.make_async_copy(lanes(k_hbm, g * D, D), kbuf.at[pl.ds(pl.multiple_of(g * R, R), R), :], loc_sem.at[0])
    c1 = pltpu.make_async_copy(lanes(v_hbm, g * D, D), vbuf.at[pl.ds(pl.multiple_of(g * R, R), R), :], loc_sem.at[1])
    c2 = pltpu.make_async_copy(lanes(k_hbm, (1 - g) * D, D), kx, loc_sem.at[2])
    c3 = pltpu.make_async_copy(lanes(v_hbm, (1 - g) * D, D), vx, loc_sem.at[3])
    c4 = pltpu.make_async_copy(lanes(q_hbm, (1 - g) * CW, CW), qx, loc_sem.at[4])
    c5 = pltpu.make_async_copy(lanes(q_hbm, g * CW, CW), qbuf.at[y], loc_sem.at[5])
    c6 = pltpu.make_async_copy(len_hbm, len_ref, loc_sem.at[6])
    c7 = pltpu.make_async_copy(sink_hbm, sink_ref, loc_sem.at[7])
    for c in (c0, c1, c2, c3, c4, c5, c6, c7):
        c.start()

    for c in (c0, c1, c2, c3):
        c.wait()
    pl.semaphore_wait(barrier, NY - 1 + 2)

    def cell(ref, slot, c):
        return ref.at[pl.ds(pl.multiple_of(slot * (2 * R) + c * R, R), R), :]

    def up_slot(zz, j):
        return j + jnp.maximum(0, j - (NZ - zz))

    def down_slot(zz, j):
        return jnp.where(zz + j >= NZ, 2 * j + 1 - (NZ - zz), NZ + j)

    def cross(slot, tslot, c, sems, j, zt, n):
        ref, sem = ((kbuf, kr_sem), (vbuf, vr_sem))[n]
        return pltpu.make_async_remote_copy(
            src_ref=cell(ref, slot, c),
            dst_ref=cell(ref, tslot, c),
            send_sem=sems[n].at[j, c],
            recv_sem=sem.at[tslot, c],
            device_id=dev(zt, y),
            device_id_type=MESH,
        )

    def up(slot, c, j, n):
        return cross(slot, up_slot(z + 1, j + 1), c, (kus, vus), j, (z + 1) % NZ, n)

    def down(slot, c, j, n):
        zt = (z + NZ - 1) % NZ
        return cross(slot, down_slot(zt, j + 1), c, (kds, vds), j, zt, n)

    def start_up(slot, c, j, n):
        @pl.when((j < NU) & (z < NZ - 1) & (z >= j))
        def _():
            up(slot, c, j, n).start()

    def start_down(slot, c, j, n):
        @pl.when((j < ND) & ((z + j) % NZ <= KD))
        def _():
            down(slot, c, j, n).start()

    for n in range(2):
        start_up(0, g, 0, n)
        start_down(0, g, 0, n)

    yp = y + 1 - 2 * g
    to_pair = (
        pltpu.make_async_remote_copy(
            src_ref=kx, dst_ref=cell(kbuf, 0, g), send_sem=xk_sem.at[0], recv_sem=kr_sem.at[0, g],
            device_id=dev(z, yp), device_id_type=MESH,
        ),
        pltpu.make_async_remote_copy(
            src_ref=vx, dst_ref=cell(vbuf, 0, g), send_sem=xk_sem.at[1], recv_sem=vr_sem.at[0, g],
            device_id=dev(z, yp), device_id_type=MESH,
        ),
    )
    for d in to_pair:
        d.start()

    def q_copy(i):
        src = qbuf.at[y] if i == 2 else qx
        return pltpu.make_async_remote_copy(
            src_ref=src, dst_ref=qbuf.at[y], send_sem=qs_sem.at[i], recv_sem=qr_sem.at[y],
            device_id=dev(z, (y + i) % NY), device_id_type=MESH,
        )

    lane = lax.broadcasted_iota(jnp.int32, (2 * R, D), 1)
    row = lax.broadcasted_iota(jnp.int32, (2 * R, D), 0)
    plain = jnp.where(lane < 64, 1.0, 0.0).astype(jnp.bfloat16)

    def fill(i, _):
        ebuf[pl.ds(pl.multiple_of(i * 2 * R, 2 * R), 2 * R), :] = plain
        return 0

    lax.fori_loop(0, NZ, fill, 0)
    c6.wait()
    c7.wait()
    kpos = row + b * 2 * R
    hit = kpos == sink_ref[0]
    for n in range(1, 4):
        hit = hit | (kpos == sink_ref[n])
    first = jnp.where(z < NU + 1, z, NZ + 1 - z)
    ebuf[pl.ds(pl.multiple_of(first * 2 * R, 2 * R), 2 * R), :] = jnp.where(
        (lane < 64) | hit, 1.0, 0.0
    ).astype(jnp.bfloat16)

    def wait_cell(slot, c, n):
        ref, sem = ((kbuf, kr_sem), (vbuf, vr_sem))[n]
        pltpu.make_async_remote_copy(
            src_ref=cell(ref, slot, c), dst_ref=cell(ref, slot, c), send_sem=xk_sem.at[0],
            recv_sem=sem.at[slot, c], device_id=dev(z, yp), device_id_type=MESH,
        ).wait_recv()

    def wait_q(t):
        pltpu.make_async_remote_copy(
            src_ref=qx, dst_ref=qbuf.at[t], send_sem=qs_sem.at[0], recv_sem=qr_sem.at[t],
            device_id=dev(z, yp), device_id_type=MESH,
        ).wait_recv()

    c4.wait()
    c5.wait()
    for i in (1, 3, 2):
        q_copy(i).start()

    for n in range(2):
        wait_cell(0, 1 - g, n)
        start_up(0, 1 - g, 0, n)
        start_down(0, 1 - g, 0, n)

    def poll(e, _):
        j = e // 2 + 1
        c = (g + e) % 2

        @pl.when((e > 0) & (e < NU))
        def _():
            pl.semaphore_wait(hello.at[e - 1], 2)

        @pl.when(e < NU - 1)
        def _():
            for zz in beside:
                pl.semaphore_signal(hello.at[e], inc=1, device_id=dev(zz, y), device_id_type=MESH)

        @pl.when((j <= NU) & (z >= j))
        def _():
            slot = up_slot(z, j)
            for n in range(2):
                wait_cell(slot, c, n)
                start_up(slot, c, j, n)

        @pl.when((j <= ND) & ((z + j) % NZ <= KD))
        def _():
            slot = down_slot(z, j)
            for n in range(2):
                wait_cell(slot, c, n)
                start_down(slot, c, j, n)

        return 0

    def scores(t, h, k):
        return lax.dot_general(
            qbuf[t, :, h * D : (h + 1) * D], k, (((1,), (1,)), ((), ())), preferred_element_type=jnp.float32
        )

    def weigh(sc, mn):
        mc = mn * LC
        cols = [jnp.exp2(sc[:, n * D : (n + 1) * D] * LC - mc) for n in range(sc.shape[1] // D)]
        return jnp.concatenate(cols, axis=1).astype(jnp.bfloat16)

    def mix(p, ve):
        return lax.dot_general(p, ve, (((1,), (0,)), ((), ())), preferred_element_type=jnp.float32)

    qi = lax.broadcasted_iota(jnp.int32, (R, 2 * R), 0)
    ki = lax.broadcasted_iota(jnp.int32, (R, 2 * R), 1)

    def attend_own(t):
        k = kbuf[0 : 2 * R, :]
        ve = jnp.concatenate([vbuf[0 : 2 * R, :], ebuf[0 : 2 * R, :]], axis=1)
        ok = ki + b * 2 * R <= qi + t * R
        sc = [jnp.where(ok, scores(t, h, k), LOW) for h in range(HG)]
        for h in range(HG):
            mn = jnp.broadcast_to(jnp.max(sc[h], axis=1, keepdims=True), (R, D))
            m_ref[t, h] = mn
            acc_ref[t, h] = mix(weigh(sc[h], mn), ve)

    def attend(t, base, n):
        rows = pl.ds(pl.multiple_of(base, 2 * R), n * 2 * R)
        k = kbuf[rows, :]
        ve = jnp.concatenate([vbuf[rows, :], ebuf[rows, :]], axis=1)
        sc = [scores(t, h, k) for h in range(HG)]
        for h in range(HG):
            mo = m_ref[t, h]
            mn = jnp.maximum(mo, jnp.max(sc[h], axis=1, keepdims=True))
            al = jnp.exp2((mo - mn) * LC)
            pv = mix(weigh(sc[h], mn), ve)
            acc_ref[t, h] = acc_ref[t, h] * jnp.concatenate([al, al], axis=1) + pv
            m_ref[t, h] = mn

    def have(st):
        j = jnp.where(st < 4, 2 * st, st + 3)
        ups = jnp.minimum(jnp.minimum(j, NU), z)
        return ups + jnp.maximum(0, jnp.minimum(j, ND) - (NZ - z) + 1)

    def item(it, e):
        k = it % 3
        st = jnp.where(it < 6, it // 3, jnp.where(it < 8, it - 6, it // 4))
        gi = jnp.where(it < 6, k + k // 2, jnp.where(it < 8, 2, gray(NY - 1 - it % 4)))
        t = (y + gi) % NY

        @pl.when(st == 0)
        def _():
            @pl.when(gi > 0)
            def _():
                wait_q(t)

            attend_own(t)

        before = have(st - 1)
        count = have(st) - before
        for n in range(1, 5):

            @pl.when((st > 0) & (count == n))
            def _():
                attend(t, (before + 1) * 2 * R, n)

        two = (it == 0) | (it == 5) | (it == 7) | (it == 11)
        one = (it == 1) | (it == 2) | (it == 9) | (it == 10)
        one = one | (it == 14) | (it == 15) | (it == 18) | (it == 19)
        polls = jnp.where(two, 2, jnp.where(one, 1, 0))
        lax.fori_loop(e, e + polls, poll, 0)
        return e + polls

    lax.fori_loop(0, 24, item, 0)

    lane1 = lax.broadcasted_iota(jnp.int32, (R, D), 1)

    def stats(t, _):
        x, m = jnp.ones((R, D), jnp.float32), jnp.zeros((R, D), jnp.float32)
        for h in range(HG):
            x = jnp.where((lane1 == h) | (lane1 == 64 + h), acc_ref[t, h, :, D : 2 * D], x)
            m = jnp.where(lane1 == h, m_ref[t, h], m)
        frac = x / pltpu.roll(x, 64, 1)
        xs_ref[...] = jnp.where(lane1 < 64, m * SCALE + jnp.log(x), frac).T
        xrecv[y, t, 0:8] = xs_ref[0:8, :]
        xrecv[y, t, 8:16] = xs_ref[64:72, :]
        return 0

    lax.fori_loop(0, NY, stats, 0)

    def tell(i):
        return pltpu.make_async_remote_copy(
            src_ref=xrecv.at[y], dst_ref=xrecv.at[y], send_sem=ss_sem.at[i], recv_sem=sr_sem.at[y],
            device_id=dev(z, (y + i) % NY), device_id_type=MESH,
        )

    def back(i):
        return pltpu.make_async_remote_copy(
            src_ref=osend.at[i], dst_ref=orecv.at[y], send_sem=os_sem.at[i], recv_sem=or_sem.at[y],
            device_id=dev(z, (y + i) % NY), device_id_type=MESH,
        )

    for i in (2, 1, 3):
        tell(i).start()

    def outputs(i, ref, at):
        t = (y + i) % NY
        for h in range(HG):
            inv = 1.0 / jnp.broadcast_to(acc_ref[t, h, :, D : D + 1], (R, D))
            ref[at, :, h * D : (h + 1) * D] = (acc_ref[t, h, :, 0:D] * inv).astype(jnp.bfloat16)

    for i in (2, 3, 1):
        outputs(i, osend, i)
    for i in (2, 3, 1):
        back(i).start()
    outputs(0, orecv, y)

    for i in range(1, NY):
        yy = (y + i) % NY
        pltpu.make_async_remote_copy(
            src_ref=xrecv.at[y], dst_ref=xrecv.at[yy], send_sem=ss_sem.at[0], recv_sem=sr_sem.at[yy],
            device_id=dev(z, yp), device_id_type=MESH,
        ).wait_recv()

    def join(gg, t):
        xa, xb = xrecv[gg, t], xrecv[2 + gg, t]
        la, lb = xa[0:8], xb[0:8]
        top = jnp.maximum(la, lb)
        ea, eb = jnp.exp(la - top), jnp.exp(lb - top)
        tot = ea + eb
        wa, wb = ea / tot, eb / tot
        pos = (z * NY + t) * R + lax.broadcasted_iota(jnp.int32, (8, D), 1)
        live = pos < len_ref[0]
        lse = jnp.where(live, top + jnp.log(tot), 0.0)
        mass = jnp.where(live, wa * xa[8:16] + wb * xb[8:16], 0.0)
        return lse, mass, jnp.where(live, wa, 0.0), jnp.where(live, wb, 0.0)

    pk_ref[...] = jnp.zeros_like(pk_ref)
    for gg in range(2):
        lse, mass = jnp.zeros((8, D), jnp.float32), jnp.zeros((8, D), jnp.float32)
        for t in range(NY):
            more = join(gg, t)
            lse, mass = lse + more[0], mass + more[1]
        pk_ref[gg * HG : (gg + 1) * HG, :] = lse[0:HG]
        pk_ref[16 + gg * HG : 16 + (gg + 1) * HG, :] = mass[0:HG]
        lse, mass, wa, wb = join(gg, y)
        lse_ref[gg * HG : (gg + 1) * HG, :] = lse[0:HG]
        mass_ref[gg * HG : (gg + 1) * HG, :] = mass[0:HG]
        pk_ref[32 + 16 * gg : 40 + 16 * gg, :] = wa
        pk_ref[40 + 16 * gg : 48 + 16 * gg, :] = wb
    xs_ref[...] = pk_ref[...].T
    zsum[z] = jnp.broadcast_to(jnp.sum(xs_ref[...], axis=0, keepdims=True), (8, D))

    def sum_z(i):
        return pltpu.make_async_remote_copy(
            src_ref=zsum.at[z], dst_ref=zsum.at[z], send_sem=zs_sem.at[i], recv_sem=zr_sem.at[z],
            device_id=dev((z + i) % NZ, y), device_id_type=MESH,
        )

    def sum_z_start(i, _):
        sum_z(i).start()
        return 0

    lax.fori_loop(1, NZ, sum_z_start, 0)

    for i in range(1, NY):
        yy = (y + i) % NY
        pltpu.make_async_remote_copy(
            src_ref=osend.at[0], dst_ref=orecv.at[yy], send_sem=os_sem.at[0], recv_sem=or_sem.at[yy],
            device_id=dev(z, yp), device_id_type=MESH,
        ).wait_recv()
    for gg in range(2):
        for h in range(HG):
            at = 32 + 16 * gg + h
            cols = slice(h * D, (h + 1) * D)
            o = xs_ref[:, at : at + 1] * orecv[gg, :, cols].astype(jnp.float32)
            o = o + xs_ref[:, at + 8 : at + 9] * orecv[2 + gg, :, cols].astype(jnp.float32)
            obuf[:, gg * CW + h * D : gg * CW + (h + 1) * D] = o.astype(jnp.bfloat16)
    places = (
        (obuf, out_hbm), (lse_ref, lse_hbm), (mass_ref, mass_hbm), (hl_ref, hl_hbm), (hs_ref, hs_hbm)
    )
    home = [pltpu.make_async_copy(a, o, loc_sem.at[n]) for n, (a, o) in enumerate(places)]
    for d in home[0:3]:
        d.start()

    def sum_z_wait(i, _):
        zz = (z + i) % NZ
        pltpu.make_async_remote_copy(
            src_ref=zsum.at[z], dst_ref=zsum.at[zz], send_sem=zs_sem.at[0], recv_sem=zr_sem.at[zz],
            device_id=dev(z, yp), device_id_type=MESH,
        ).wait_recv()
        return 0

    lax.fori_loop(1, NZ, sum_z_wait, 0)
    total = zsum[0]
    for i in range(1, NZ):
        total = total + zsum[i]
    mean = total[0:1, :] / len_ref[0].astype(jnp.float32)
    hl_ref[...] = mean[:, 0 : 2 * HG]
    hs_ref[...] = mean[:, 16 : 16 + 2 * HG]

    for d in home[3:5]:
        d.start()

    for c in range(2):
        for j in range(NU):

            @pl.when((z < NZ - 1) & (z >= j))
            def _():
                for n in range(2):
                    up(0, c, j, n).wait_send()

        for j in range(ND):

            @pl.when((z + j) % NZ <= KD)
            def _():
                for n in range(2):
                    down(0, c, j, n).wait_send()

    for d in to_pair:
        d.wait_send()
    for i in (1, 3, 2):
        q_copy(i).wait_send()
        tell(i).wait_send()
        back(i).wait_send()

    def sum_z_sent(i, _):
        sum_z(i).wait_send()
        return 0

    lax.fori_loop(1, NZ, sum_z_sent, 0)
    for d in home:
        d.wait()


def hand_on(*refs):
    n = (len(refs) - 2) // 3
    ins, outs, held = refs[:n], refs[n : 2 * n], refs[2 * n : 3 * n]
    come, go = refs[3 * n :]
    for i in range(n):
        pltpu.make_async_copy(ins[i], held[i], come.at[i]).start()
    for i in range(n):
        pltpu.make_async_copy(ins[i], held[i], come.at[i]).wait()
        pltpu.make_async_copy(held[i], outs[i], go.at[i]).start()
    for i in range(n):
        pltpu.make_async_copy(held[i], outs[i], go.at[i]).wait()


def body(queries, keys, values, doc_length, sink_pos):
    NZ = lax.axis_size("seq") // NY
    NU = NZ // 2
    cells = NZ + NU
    f32, bf16 = jnp.float32, jnp.bfloat16
    vm, dma = pltpu.VMEM, pltpu.SemaphoreType.DMA
    results = (
        jax.ShapeDtypeStruct((R, 2 * CW), bf16),
        jax.ShapeDtypeStruct((2 * HG, R), f32),
        jax.ShapeDtypeStruct((2 * HG, R), f32),
        jax.ShapeDtypeStruct((1, 2 * HG), f32),
        jax.ShapeDtypeStruct((1, 2 * HG), f32),
    )
    parts = pl.pallas_call(
        functools.partial(kernel, NZ),
        out_shape=results,
        in_specs=[
            pl.BlockSpec(memory_space=pl.ANY),
            pl.BlockSpec(memory_space=pl.ANY),
            pl.BlockSpec(memory_space=pl.ANY),
            pl.BlockSpec(memory_space=pl.ANY),
            pl.BlockSpec(memory_space=pl.ANY),
        ],
        out_specs=(pl.BlockSpec(memory_space=pl.ANY),) * 5,
        scratch_shapes=[
            pltpu.SMEM((1,), jnp.int32),
            pltpu.SMEM((4,), jnp.int32),
            vm((2 * HG, R), f32),
            vm((2 * HG, R), f32),
            vm((1, 2 * HG), f32),
            vm((1, 2 * HG), f32),
            vm((NY, R, CW), bf16),
            vm((R, CW), bf16),
            vm((cells * 2 * R, D), bf16),
            vm((cells * 2 * R, D), bf16),
            vm((R, D), bf16),
            vm((R, D), bf16),
            vm((NZ * 2 * R, D), bf16),
            vm((NY, HG, R, D), f32),
            vm((NY, HG, R, 2 * D), f32),
            vm((NY, R, CW), bf16),
            vm((NY, R, CW), bf16),
            vm((R, 2 * CW), bf16),
            vm((NY, NY, 16, R), f32),
            vm((D, R), f32),
            vm((D, R), f32),
            vm((NZ, 8, D), f32),
            dma((8,)),
            dma((NY,)),
            dma((NY,)),
            dma((2,)),
            dma((cells, 2)),
            dma((cells, 2)),
            dma((NU, 2)),
            dma((NU, 2)),
            dma((NU, 2)),
            dma((NU, 2)),
            dma((NY,)),
            dma((NY,)),
            dma((NY,)),
            dma((NY,)),
            dma((NZ,)),
            dma((NZ,)),
            pltpu.SemaphoreType.REGULAR((NU - 1,)),
        ],
        compiler_params=pltpu.CompilerParams(
            collective_id=0, has_side_effects=True, vmem_limit_bytes=56 * 2**20
        ),
    )(doc_length, sink_pos, queries, keys, values)
    out, lse, mass, hl, hs = pl.pallas_call(
        hand_on,
        out_shape=results,
        in_specs=[pl.BlockSpec(memory_space=pl.ANY)] * 5,
        out_specs=(pl.BlockSpec(memory_space=pl.ANY),) * 5,
        scratch_shapes=[vm(r.shape, r.dtype) for r in results] + [dma((5,)), dma((5,))],
    )(*parts)
    return out, lse, mass, hl.reshape(2 * HG), hs.reshape(2 * HG)


def solution(mesh):
    rows = P(("doc", "seq"), None)
    return jax.shard_map(
        body,
        mesh=mesh,
        in_specs=(rows, rows, rows, P("doc"), P("doc")),
        out_specs=(rows, P(None, ("doc", "seq")), P(None, ("doc", "seq")), P("doc"), P("doc")),
        check_vma=False,
    )
```

time: 79.5 us -> 69.9 us (0.88)
  Pallas kernels: 73.7 us -> 68.4 us
  local copies, waits for them, and re-layouts: 4.26 us -> 0 us
    pallas_call x1 -> x2, Pallas kernels: 73.7 us -> 68.4 us  [the longest x1 66.5 us: body(): pl.pallas_call(functools.partial(kernel, NZ), out_shape=results, in_specs...]
    unnamed x13 -> x0, local copies, waits for them, and re-layouts: 4.26 us -> none
where the time goes in v2:
time: 69.9 us; the launch traced here: 69.7 us
  Pallas kernels  68.4 us (98%)
  between operations  1.29 us (2%)
    pallas_call x1, Pallas kernels, body(): pl.pallas_call(functools.partial(kernel, NZ), out_shape=results, in_specs...  66.5 us
    pallas_call x1, Pallas kernels, body(): pl.pallas_call(hand_on, out_shape=results, in_specs=[pl.BlockSpec(memory_...  1.88 us

profile of v2, /device:TPU:6, one launch (start us, length us, event | category | flops | bytes accessed | tf_op | source)
XLA Modules:
  0.0 69.7 jit_solution(15381785435503803950)
XLA Ops:
  1.3 66.5 %shard_map.92 = (bf16[128,1792]{1,0:T(8,128)(2,1)}, f32[14,128]{1,0:T(8,128)}, f32[14,128]{1,0:T(8,128)}, f32[1,14]{1,0:T(1,128)}, f32[1,14]{1,0:T(1,128)}) custom-call(s32[1]{0:T(128)S(6)} %copy.10.len_hbm, s32[4]{0:T(128)} %sink_hbm.1, bf16[128,1792]{1,0:T(8,128)(2,1)} %q_hbm.1, bf16[128,256]{1,0:T(8,128)(2,1)} %k_hbm.1, bf16[128,256]{1,0:T(8,128)(2,1)} %v_hbm.1), custom_call_target="tpu_custom_call" | custom-call | tf_op jit(solution)/shard_map/pallas_call | solution.py:511
  67.8 1.9 %shard_map.93 = (bf16[128,1792]{1,0:T(8,128)(2,1)}, f32[14,128]{1,0:T(8,128)}, f32[14,128]{1,0:T(8,128)}, f32[1,14]{1,0:T(1,128)}, f32[1,14]{1,0:T(1,128)}) custom-call(bf16[128,1792]{1,0:T(8,128)(2,1)} %get-tuple-element.15.refs_0_, f32[14,128]{1,0:T(8,128)} %get-tuple-element.16.refs_1_, f32[14,128]{1,0:T(8,128)} %get-tuple-element.17.refs_2_, ...), custom_call_target="tpu_custom_call" | custom-call | tf_op jit(solution)/shard_map/pallas_call | solution.py:567

commit v3 on v2

--- a/solution.py
+++ b/solution.py
@@ -18,8 +18,42 @@
 LOW = -(2.0**60)
 
 
-def gray(i):
-    return i + (i // 2) * (1 - 2 * (i % 2))
+PLAN = (
+    (0, 0, 0, 2),
+    (0, 0, 1, 0),
+    (1, 0, 0, 0),
+    (1, 0, 1, 1),
+    (3, 0, 0, 1),
+    (3, 0, 2, 0),
+    (0, 1, 2, 1),
+    (1, 1, 2, 1),
+    (2, 0, 0, 0),
+    (2, 0, 2, 1),
+    (0, 2, 3, 1),
+    (1, 2, 4, 0),
+    (2, 2, 4, 1),
+    (3, 2, 4, 1),
+    (0, 3, 5, 1),
+    (1, 4, 5, 1),
+    (2, 4, 6, 0),
+    (3, 4, 6, 1),
+    (0, 5, 6, 1),
+    (1, 5, 7, 0),
+    (0, 6, 7, 2),
+    (2, 6, 8, 0),
+    (3, 6, 8, 0),
+    (1, 7, 8, 0),
+    (0, 7, 8, 0),
+)
+assert sum(row[3] for row in PLAN) == 16
+
+
+def pick(i, table):
+    at = jnp.int32(table[0])
+    for n in range(1, len(table)):
+        if table[n] != table[n - 1]:
+            at = at + jnp.where(i >= n, table[n] - table[n - 1], 0)
+    return at
 
 
 def kernel(
@@ -62,10 +96,8 @@
     xk_sem,
     kr_sem,
     vr_sem,
-    kus,
-    vus,
-    kds,
-    vds,
+    us_sem,
+    ds_sem,
     os_sem,
     or_sem,
     ss_sem,
@@ -122,23 +154,23 @@
     def down_slot(zz, j):
         return jnp.where(zz + j >= NZ, 2 * j + 1 - (NZ - zz), NZ + j)
 
-    def cross(slot, tslot, c, sems, j, zt, n):
+    def cross(slot, tslot, c, sent, j, zt, n):
         ref, sem = ((kbuf, kr_sem), (vbuf, vr_sem))[n]
         return pltpu.make_async_remote_copy(
             src_ref=cell(ref, slot, c),
             dst_ref=cell(ref, tslot, c),
-            send_sem=sems[n].at[j, c],
+            send_sem=sent.at[j],
             recv_sem=sem.at[tslot, c],
             device_id=dev(zt, y),
             device_id_type=MESH,
         )
 
     def up(slot, c, j, n):
-        return cross(slot, up_slot(z + 1, j + 1), c, (kus, vus), j, (z + 1) % NZ, n)
+        return cross(slot, up_slot(z + 1, j + 1), c, us_sem, j, (z + 1) % NZ, n)
 
     def down(slot, c, j, n):
         zt = (z + NZ - 1) % NZ
-        return cross(slot, down_slot(zt, j + 1), c, (kds, vds), j, zt, n)
+        return cross(slot, down_slot(zt, j + 1), c, ds_sem, j, zt, n)
 
     def start_up(slot, c, j, n):
         @pl.when((j < NU) & (z < NZ - 1) & (z >= j))
@@ -157,11 +189,11 @@
     yp = y + 1 - 2 * g
     to_pair = (
         pltpu.make_async_remote_copy(
-            src_ref=kx, dst_ref=cell(kbuf, 0, g), send_sem=xk_sem.at[0], recv_sem=kr_sem.at[0, g],
+            src_ref=kx, dst_ref=cell(kbuf, 0, g), send_sem=xk_sem, recv_sem=kr_sem.at[0, g],
             device_id=dev(z, yp), device_id_type=MESH,
         ),
         pltpu.make_async_remote_copy(
-            src_ref=vx, dst_ref=cell(vbuf, 0, g), send_sem=xk_sem.at[1], recv_sem=vr_sem.at[0, g],
+            src_ref=vx, dst_ref=cell(vbuf, 0, g), send_sem=xk_sem, recv_sem=vr_sem.at[0, g],
             device_id=dev(z, yp), device_id_type=MESH,
         ),
     )
@@ -171,7 +203,7 @@
     def q_copy(i):
         src = qbuf.at[y] if i == 2 else qx
         return pltpu.make_async_remote_copy(
-            src_ref=src, dst_ref=qbuf.at[y], send_sem=qs_sem.at[i], recv_sem=qr_sem.at[y],
+            src_ref=src, dst_ref=qbuf.at[y], send_sem=qs_sem, recv_sem=qr_sem.at[y],
             device_id=dev(z, (y + i) % NY), device_id_type=MESH,
         )
 
@@ -198,13 +230,13 @@
     def wait_cell(slot, c, n):
         ref, sem = ((kbuf, kr_sem), (vbuf, vr_sem))[n]
         pltpu.make_async_remote_copy(
-            src_ref=cell(ref, slot, c), dst_ref=cell(ref, slot, c), send_sem=xk_sem.at[0],
+            src_ref=cell(ref, slot, c), dst_ref=cell(ref, slot, c), send_sem=xk_sem,
             recv_sem=sem.at[slot, c], device_id=dev(z, yp), device_id_type=MESH,
         ).wait_recv()
 
     def wait_q(t):
         pltpu.make_async_remote_copy(
-            src_ref=qx, dst_ref=qbuf.at[t], send_sem=qs_sem.at[0], recv_sem=qr_sem.at[t],
+            src_ref=qx, dst_ref=qbuf.at[t], send_sem=qs_sem, recv_sem=qr_sem.at[t],
             device_id=dev(z, yp), device_id_type=MESH,
         ).wait_recv()
 
@@ -286,18 +318,16 @@
             acc_ref[t, h] = acc_ref[t, h] * jnp.concatenate([al, al], axis=1) + pv
             m_ref[t, h] = mn
 
-    def have(st):
-        j = jnp.where(st < 4, 2 * st, st + 3)
+    def have(j):
         ups = jnp.minimum(jnp.minimum(j, NU), z)
         return ups + jnp.maximum(0, jnp.minimum(j, ND) - (NZ - z) + 1)
 
     def item(it, e):
-        k = it % 3
-        st = jnp.where(it < 6, it // 3, jnp.where(it < 8, it - 6, it // 4))
-        gi = jnp.where(it < 6, k + k // 2, jnp.where(it < 8, 2, gray(NY - 1 - it % 4)))
+        row = pick(it, [a + 4 * (p + 4 * (j0 + 16 * j1)) for a, j0, j1, p in PLAN])
+        gi, polls, j0, j1 = row % 4, row // 4 % 4, row // 16 % 16, row // 256
         t = (y + gi) % NY
 
-        @pl.when(st == 0)
+        @pl.when(j1 == 0)
         def _():
             @pl.when(gi > 0)
             def _():
@@ -305,22 +335,18 @@
 
             attend_own(t)
 
-        before = have(st - 1)
-        count = have(st) - before
+        before = have(j0)
+        count = have(j1) - before
         for n in range(1, 5):
 
-            @pl.when((st > 0) & (count == n))
+            @pl.when((j1 > 0) & (count == n))
             def _():
                 attend(t, (before + 1) * 2 * R, n)
 
-        two = (it == 0) | (it == 5) | (it == 7) | (it == 11)
-        one = (it == 1) | (it == 2) | (it == 9) | (it == 10)
-        one = one | (it == 14) | (it == 15) | (it == 18) | (it == 19)
-        polls = jnp.where(two, 2, jnp.where(one, 1, 0))
         lax.fori_loop(e, e + polls, poll, 0)
         return e + polls
 
-    lax.fori_loop(0, 24, item, 0)
+    lax.fori_loop(0, len(PLAN), item, 0)
 
     lane1 = lax.broadcasted_iota(jnp.int32, (R, D), 1)
 
@@ -339,13 +365,13 @@
 
     def tell(i):
         return pltpu.make_async_remote_copy(
-            src_ref=xrecv.at[y], dst_ref=xrecv.at[y], send_sem=ss_sem.at[i], recv_sem=sr_sem.at[y],
+            src_ref=xrecv.at[y], dst_ref=xrecv.at[y], send_sem=ss_sem, recv_sem=sr_sem,
             device_id=dev(z, (y + i) % NY), device_id_type=MESH,
         )
 
     def back(i):
         return pltpu.make_async_remote_copy(
-            src_ref=osend.at[i], dst_ref=orecv.at[y], send_sem=os_sem.at[i], recv_sem=or_sem.at[y],
+            src_ref=osend.at[i], dst_ref=orecv.at[y], send_sem=os_sem, recv_sem=or_sem,
             device_id=dev(z, (y + i) % NY), device_id_type=MESH,
         )
 
@@ -364,12 +390,12 @@
         back(i).start()
     outputs(0, orecv, y)
 
-    for i in range(1, NY):
-        yy = (y + i) % NY
+    def landed(ref, sem):
         pltpu.make_async_remote_copy(
-            src_ref=xrecv.at[y], dst_ref=xrecv.at[yy], send_sem=ss_sem.at[0], recv_sem=sr_sem.at[yy],
-            device_id=dev(z, yp), device_id_type=MESH,
+            src_ref=ref, dst_ref=ref, send_sem=xk_sem, recv_sem=sem, device_id=dev(z, yp), device_id_type=MESH
         ).wait_recv()
+
+    landed(xrecv.at[0 : NY - 1], sr_sem)
 
     def join(gg, t):
         xa, xb = xrecv[gg, t], xrecv[2 + gg, t]
@@ -402,7 +428,7 @@
 
     def sum_z(i):
         return pltpu.make_async_remote_copy(
-            src_ref=zsum.at[z], dst_ref=zsum.at[z], send_sem=zs_sem.at[i], recv_sem=zr_sem.at[z],
+            src_ref=zsum.at[z], dst_ref=zsum.at[z], send_sem=zs_sem, recv_sem=zr_sem,
             device_id=dev((z + i) % NZ, y), device_id_type=MESH,
         )
 
@@ -412,12 +438,7 @@
 
     lax.fori_loop(1, NZ, sum_z_start, 0)
 
-    for i in range(1, NY):
-        yy = (y + i) % NY
-        pltpu.make_async_remote_copy(
-            src_ref=osend.at[0], dst_ref=orecv.at[yy], send_sem=os_sem.at[0], recv_sem=or_sem.at[yy],
-            device_id=dev(z, yp), device_id_type=MESH,
-        ).wait_recv()
+    landed(orecv.at[0 : NY - 1], or_sem)
     for gg in range(2):
         for h in range(HG):
             at = 32 + 16 * gg + h
@@ -432,15 +453,7 @@
     for d in home[0:3]:
         d.start()
 
-    def sum_z_wait(i, _):
-        zz = (z + i) % NZ
-        pltpu.make_async_remote_copy(
-            src_ref=zsum.at[z], dst_ref=zsum.at[zz], send_sem=zs_sem.at[0], recv_sem=zr_sem.at[zz],
-            device_id=dev(z, yp), device_id_type=MESH,
-        ).wait_recv()
-        return 0
-
-    lax.fori_loop(1, NZ, sum_z_wait, 0)
+    landed(zsum.at[0 : NZ - 1], zr_sem)
     total = zsum[0]
     for i in range(1, NZ):
         total = total + zsum[i]
@@ -451,33 +464,28 @@
     for d in home[3:5]:
         d.start()
 
-    for c in range(2):
-        for j in range(NU):
-
-            @pl.when((z < NZ - 1) & (z >= j))
-            def _():
-                for n in range(2):
-                    up(0, c, j, n).wait_send()
-
-        for j in range(ND):
-
-            @pl.when((z + j) % NZ <= KD)
-            def _():
-                for n in range(2):
-                    down(0, c, j, n).wait_send()
-
-    for d in to_pair:
-        d.wait_send()
-    for i in (1, 3, 2):
-        q_copy(i).wait_send()
-        tell(i).wait_send()
-        back(i).wait_send()
-
-    def sum_z_sent(i, _):
-        sum_z(i).wait_send()
-        return 0
-
-    lax.fori_loop(1, NZ, sum_z_sent, 0)
+    def left(ref, sem):
+        pltpu.make_async_remote_copy(
+            src_ref=ref, dst_ref=ref, send_sem=sem, recv_sem=xk_sem, device_id=dev(z, yp), device_id_type=MESH
+        ).wait_send()
+
+    for j in range(NU):
+
+        @pl.when((z < NZ - 1) & (z >= j))
+        def _():
+            left(kbuf.at[0 : 4 * R, :], us_sem.at[j])
+
+    for j in range(ND):
+
+        @pl.when((z + j) % NZ <= KD)
+        def _():
+            left(kbuf.at[0 : 4 * R, :], ds_sem.at[j])
+
+    left(kbuf.at[0 : 2 * R, :], xk_sem)
+    left(qbuf.at[0 : NY - 1], qs_sem)
+    left(xrecv.at[0 : NY - 1], ss_sem)
+    left(osend.at[0 : NY - 1], os_sem)
+    left(zsum.at[0 : NZ - 1], zs_sem)
     for d in home:
         d.wait()
 
@@ -543,21 +551,19 @@
             vm((D, R), f32),
             vm((NZ, 8, D), f32),
             dma((8,)),
+            dma,
             dma((NY,)),
-            dma((NY,)),
-            dma((2,)),
+            dma,
             dma((cells, 2)),
             dma((cells, 2)),
-            dma((NU, 2)),
-            dma((NU, 2)),
-            dma((NU, 2)),
-            dma((NU, 2)),
-            dma((NY,)),
-            dma((NY,)),
-            dma((NY,)),
-            dma((NY,)),
-            dma((NZ,)),
-            dma((NZ,)),
+            dma((NU,)),
+            dma((NU,)),
+            dma,
+            dma,
+            dma,
+            dma,
+            dma,
+            dma,
             pltpu.SemaphoreType.REGULAR((NU - 1,)),
         ],
         compiler_params=pltpu.CompilerParams(

time: 69.9 us -> 67.2 us (0.961)
  Pallas kernels: 68.4 us -> 65.2 us
    pallas_call x1, Pallas kernels: 66.5 us -> 63.4 us  [body(): pl.pallas_call(functools.partial(kernel, NZ), out_shape=results, in_specs...]
where the time goes in v3:
time: 67.2 us; the launch traced here: 66.5 us
  Pallas kernels  65.2 us (97%)
  between operations  1.29 us (2%)
    pallas_call x1, Pallas kernels, body(): pl.pallas_call(functools.partial(kernel, NZ), out_shape=results, in_specs...  63.4 us
    pallas_call x1, Pallas kernels, body(): pl.pallas_call(hand_on, out_shape=results, in_specs=[pl.BlockSpec(memory_...  1.88 us

profile of v3, /device:TPU:6, one launch (start us, length us, event | category | flops | bytes accessed | tf_op | source)
XLA Modules:
  0.0 66.5 jit_solution(6879770221395768344)
XLA Ops:
  1.3 63.4 %shard_map.92 = (bf16[128,1792]{1,0:T(8,128)(2,1)}, f32[14,128]{1,0:T(8,128)}, f32[14,128]{1,0:T(8,128)}, f32[1,14]{1,0:T(1,128)}, f32[1,14]{1,0:T(1,128)}) custom-call(s32[1]{0:T(128)S(6)} %copy.10.len_hbm, s32[4]{0:T(128)} %sink_hbm.1, bf16[128,1792]{1,0:T(8,128)(2,1)} %q_hbm.1, bf16[128,256]{1,0:T(8,128)(2,1)} %k_hbm.1, bf16[128,256]{1,0:T(8,128)(2,1)} %v_hbm.1), custom_call_target="tpu_custom_call" | custom-call | tf_op jit(solution)/shard_map/pallas_call | solution.py:519
  64.6 1.9 %shard_map.93 = (bf16[128,1792]{1,0:T(8,128)(2,1)}, f32[14,128]{1,0:T(8,128)}, f32[14,128]{1,0:T(8,128)}, f32[1,14]{1,0:T(1,128)}, f32[1,14]{1,0:T(1,128)}) custom-call(bf16[128,1792]{1,0:T(8,128)(2,1)} %get-tuple-element.15.refs_0_, f32[14,128]{1,0:T(8,128)} %get-tuple-element.16.refs_1_, f32[14,128]{1,0:T(8,128)} %get-tuple-element.17.refs_2_, ...), custom_call_target="tpu_custom_call" | custom-call | tf_op jit(solution)/shard_map/pallas_call | solution.py:573

commit v4 on v3

--- a/solution.py
+++ b/solution.py
@@ -129,6 +129,8 @@
         pl.semaphore_signal(barrier, inc=1, device_id=dev(zz, y), device_id_type=MESH)
     for i in range(1, NY):
         pl.semaphore_signal(barrier, inc=1, device_id=dev(z, (y + i) % NY), device_id_type=MESH)
+    yp = y + 1 - 2 * g
+    pl.semaphore_signal(barrier, inc=1, device_id=dev(beside[1], yp), device_id_type=MESH)
 
     c0 = pltpu.make_async_copy(lanes(k_hbm, g * D, D), kbuf.at[pl.ds(pl.multiple_of(g * R, R), R), :], loc_sem.at[0])
     c1 = pltpu.make_async_copy(lanes(v_hbm, g * D, D), vbuf.at[pl.ds(pl.multiple_of(g * R, R), R), :], loc_sem.at[1])
@@ -143,7 +145,7 @@
 
     for c in (c0, c1, c2, c3):
         c.wait()
-    pl.semaphore_wait(barrier, NY - 1 + 2)
+    pl.semaphore_wait(barrier, NY - 1 + 3)
 
     def cell(ref, slot, c):
         return ref.at[pl.ds(pl.multiple_of(slot * (2 * R) + c * R, R), R), :]
@@ -186,7 +188,6 @@
         start_up(0, g, 0, n)
         start_down(0, g, 0, n)
 
-    yp = y + 1 - 2 * g
     to_pair = (
         pltpu.make_async_remote_copy(
             src_ref=kx, dst_ref=cell(kbuf, 0, g), send_sem=xk_sem, recv_sem=kr_sem.at[0, g],
@@ -200,6 +201,14 @@
     for d in to_pair:
         d.start()
 
+    @pl.when(z < NZ - 1)
+    def _():
+        for ref, dst, sem in ((kx, kbuf, kr_sem), (vx, vbuf, vr_sem)):
+            pltpu.make_async_remote_copy(
+                src_ref=ref, dst_ref=cell(dst, up_slot(z + 1, 1), g), send_sem=us_sem.at[0],
+                recv_sem=sem.at[up_slot(z + 1, 1), g], device_id=dev((z + 1) % NZ, yp), device_id_type=MESH,
+            ).start()
+
     def q_copy(i):
         src = qbuf.at[y] if i == 2 else qx
         return pltpu.make_async_remote_copy(
@@ -247,21 +256,11 @@
 
     for n in range(2):
         wait_cell(0, 1 - g, n)
-        start_up(0, 1 - g, 0, n)
         start_down(0, 1 - g, 0, n)
 
     def poll(e, _):
         j = e // 2 + 1
         c = (g + e) % 2
-
-        @pl.when((e > 0) & (e < NU))
-        def _():
-            pl.semaphore_wait(hello.at[e - 1], 2)
-
-        @pl.when(e < NU - 1)
-        def _():
-            for zz in beside:
-                pl.semaphore_signal(hello.at[e], inc=1, device_id=dev(zz, y), device_id_type=MESH)
 
         @pl.when((j <= NU) & (z >= j))
         def _():
@@ -276,6 +275,17 @@
             for n in range(2):
                 wait_cell(slot, c, n)
                 start_down(slot, c, j, n)
+
+        r = e // 2
+
+        @pl.when((e % 2 == 0) & (r > 0) & (r < NU))
+        def _():
+            pl.semaphore_wait(hello.at[r - 1], 2)
+
+        @pl.when((e % 2 == 0) & (r < NU - 1))
+        def _():
+            for zz in beside:
+                pl.semaphore_signal(hello.at[r], inc=1, device_id=dev(zz, y), device_id_type=MESH)
 
         return 0
 
@@ -325,6 +335,7 @@
     def item(it, e):
         row = pick(it, [a + 4 * (p + 4 * (j0 + 16 * j1)) for a, j0, j1, p in PLAN])
         gi, polls, j0, j1 = row % 4, row // 4 % 4, row // 16 % 16, row // 256
+        gi = jnp.where((gi % 2 == 1) & (g == 0), 4 - gi, gi)
         t = (y + gi) % NY
 
         @pl.when(j1 == 0)

time: 67.2 us -> 66.1 us (0.984)
  no operation moved by 1% of the time
where the time goes in v4:
time: 66.1 us; the launch traced here: 65.9 us
  Pallas kernels  64.6 us (98%)
  between operations  1.29 us (2%)
    pallas_call x1, Pallas kernels, body(): pl.pallas_call(functools.partial(kernel, NZ), out_shape=results, in_specs...  62.7 us
    pallas_call x1, Pallas kernels, body(): pl.pallas_call(hand_on, out_shape=results, in_specs=[pl.BlockSpec(memory_...  1.88 us

profile of v4, /device:TPU:6, one launch (start us, length us, event | category | flops | bytes accessed | tf_op | source)
XLA Modules:
  0.0 65.9 jit_solution(13810773231005909999)
XLA Ops:
  1.3 62.7 %shard_map.92 = (bf16[128,1792]{1,0:T(8,128)(2,1)}, f32[14,128]{1,0:T(8,128)}, f32[14,128]{1,0:T(8,128)}, f32[1,14]{1,0:T(1,128)}, f32[1,14]{1,0:T(1,128)}) custom-call(s32[1]{0:T(128)S(6)} %copy.10.len_hbm, s32[4]{0:T(128)} %sink_hbm.1, bf16[128,1792]{1,0:T(8,128)(2,1)} %q_hbm.1, bf16[128,256]{1,0:T(8,128)(2,1)} %k_hbm.1, bf16[128,256]{1,0:T(8,128)(2,1)} %v_hbm.1), custom_call_target="tpu_custom_call" | custom-call | tf_op jit(solution)/shard_map/pallas_call | solution.py:530
  64.0 1.9 %shard_map.93 = (bf16[128,1792]{1,0:T(8,128)(2,1)}, f32[14,128]{1,0:T(8,128)}, f32[14,128]{1,0:T(8,128)}, f32[1,14]{1,0:T(1,128)}, f32[1,14]{1,0:T(1,128)}) custom-call(bf16[128,1792]{1,0:T(8,128)(2,1)} %get-tuple-element.15.refs_0_, f32[14,128]{1,0:T(8,128)} %get-tuple-element.16.refs_1_, f32[14,128]{1,0:T(8,128)} %get-tuple-element.17.refs_2_, ...), custom_call_target="tpu_custom_call" | custom-call | tf_op jit(solution)/shard_map/pallas_call | solution.py:584

commit v5 on v4

--- a/solution.py
+++ b/solution.py
@@ -36,10 +36,9 @@
     (0, 3, 5, 1),
     (1, 4, 5, 1),
     (2, 4, 6, 0),
-    (3, 4, 6, 1),
-    (0, 5, 6, 1),
+    (3, 4, 6, 2),
     (1, 5, 7, 0),
-    (0, 6, 7, 2),
+    (0, 5, 7, 2),
     (2, 6, 8, 0),
     (3, 6, 8, 0),
     (1, 7, 8, 0),

time: 66.1 us -> 66.1 us (level)
  no operation moved by 1% of the time
where the time goes in v5:
time: 66.1 us; the launch traced here: 65.9 us
  Pallas kernels  64.6 us (98%)
  between operations  1.29 us (2%)
    pallas_call x1, Pallas kernels, body(): pl.pallas_call(functools.partial(kernel, NZ), out_shape=results, in_specs...  62.8 us
    pallas_call x1, Pallas kernels, body(): pl.pallas_call(hand_on, out_shape=results, in_specs=[pl.BlockSpec(memory_...  1.88 us

profile of v5, /device:TPU:6, one launch (start us, length us, event | category | flops | bytes accessed | tf_op | source)
XLA Modules:
  0.0 65.9 jit_solution(10655247607050467462)
XLA Ops:
  1.3 62.8 %shard_map.92 = (bf16[128,1792]{1,0:T(8,128)(2,1)}, f32[14,128]{1,0:T(8,128)}, f32[14,128]{1,0:T(8,128)}, f32[1,14]{1,0:T(1,128)}, f32[1,14]{1,0:T(1,128)}) custom-call(s32[1]{0:T(128)S(6)} %copy.10.len_hbm, s32[4]{0:T(128)} %sink_hbm.1, bf16[128,1792]{1,0:T(8,128)(2,1)} %q_hbm.1, bf16[128,256]{1,0:T(8,128)(2,1)} %k_hbm.1, bf16[128,256]{1,0:T(8,128)(2,1)} %v_hbm.1), custom_call_target="tpu_custom_call" | custom-call | tf_op jit(solution)/shard_map/pallas_call | solution.py:529
  64.1 1.9 %shard_map.93 = (bf16[128,1792]{1,0:T(8,128)(2,1)}, f32[14,128]{1,0:T(8,128)}, f32[14,128]{1,0:T(8,128)}, f32[1,14]{1,0:T(1,128)}, f32[1,14]{1,0:T(1,128)}) custom-call(bf16[128,1792]{1,0:T(8,128)(2,1)} %get-tuple-element.15.refs_0_, f32[14,128]{1,0:T(8,128)} %get-tuple-element.16.refs_1_, f32[14,128]{1,0:T(8,128)} %get-tuple-element.17.refs_2_, ...), custom_call_target="tpu_custom_call" | custom-call | tf_op jit(solution)/shard_map/pallas_call | solution.py:583
